TPU v7x, 32 devices: a whole 2x2x4 slice. The times are simulated.
32 devices in a mesh: freq: 4 (over y, x), row: 8 (over z, core).
Axes of the slice: x: 2, y: 2, z: 4, core: 2. Of those that a mesh axis runs over, the one named last changes fastest.
Arguments:
- data: bfloat16 [4, 2, 2048, 2048], P('freq', None, 'row'), may hold values from -60 to 60
Outputs:
- solution: float32 [4, 2, 2048, 2048], P('freq', None, 'row')
- direction: float32 [4, 2, 2048, 2048], P('freq', None, 'row')
All inputs are finite; a program needn't handle non-finite values.
Results may differ from a plain program's by a relative error of at most 0.0042.
Values may be sent and summed in bfloat16 or wider, within the bound.
A program may use at most 128 MiB of HBM per device.

v0:
```python
import jax
import jax.numpy as jnp
from jax import lax
from jax.sharding import PartitionSpec as P

ITERS = 2


def times_data(rounded, block):
    real_part = jnp.einsum(
        "frk,fkn->frn", rounded[:, 0], block[:, 0], preferred_element_type=jnp.float32
    ) - jnp.einsum("frk,fkn->frn", rounded[:, 1], block[:, 1], preferred_element_type=jnp.float32)
    imag_part = jnp.einsum(
        "frk,fkn->frn", rounded[:, 0], block[:, 1], preferred_element_type=jnp.float32
    ) + jnp.einsum("frk,fkn->frn", rounded[:, 1], block[:, 0], preferred_element_type=jnp.float32)
    return jnp.stack([real_part, imag_part], axis=1)


def times_adjoint(rounded, block):
    real_part = jnp.einsum(
        "frk,fnk->frn", rounded[:, 0], block[:, 0], preferred_element_type=jnp.float32
    ) + jnp.einsum("frk,fnk->frn", rounded[:, 1], block[:, 1], preferred_element_type=jnp.float32)
    imag_part = jnp.einsum(
        "frk,fnk->frn", rounded[:, 1], block[:, 0], preferred_element_type=jnp.float32
    ) - jnp.einsum("frk,fnk->frn", rounded[:, 0], block[:, 1], preferred_element_type=jnp.float32)
    return jnp.stack([real_part, imag_part], axis=1)


def on_device(data):
    order = data.shape[3]
    weight = 1.0 / (3.0 * (2.0 * order) ** 0.5)
    observed = data.astype(jnp.float32)
    zeros = jnp.zeros_like(observed)
    whole = lax.all_gather(data, "row", axis=2, tiled=True)
    first_image = observed - weight * times_adjoint(observed.astype(jnp.bfloat16), whole)

    def pair_step(data_raw, model_unit, image):
        data_sq, image_sq, cross, model_sq = lax.psum(
            (
                jnp.sum(data_raw * data_raw),
                jnp.sum(image * image),
                jnp.sum(image * model_unit),
                jnp.sum(model_unit * model_unit),
            ),
            ("freq", "row"),
        )
        beta_now = jnp.sqrt(data_sq)
        model_raw = image / beta_now - beta_now * model_unit
        alpha_now = jnp.sqrt(
            image_sq / (beta_now * beta_now) - 2.0 * cross + beta_now * beta_now * model_sq
        )
        return (beta_now, data_raw / beta_now, model_raw, alpha_now, model_raw / alpha_now)

    beta_now, data_unit, model_raw, alpha_now, model_unit = pair_step(observed, zeros, first_image)
    solution = zeros
    direction = model_unit
    phi_bar = beta_now
    rho_bar = alpha_now
    for iteration in range(ITERS):
        data_raw = (
            model_raw - weight * times_data(model_raw.astype(jnp.bfloat16), whole)
        ) / alpha_now - alpha_now * data_unit
        beta_now, data_unit, model_raw, alpha_now, model_unit = pair_step(
            data_raw,
            model_unit,
            data_raw - weight * times_adjoint(data_raw.astype(jnp.bfloat16), whole),
        )
        rho_value = jnp.sqrt(rho_bar * rho_bar + beta_now * beta_now)
        cosine = rho_bar / rho_value
        sine_value = beta_now / rho_value
        theta_value = sine_value * alpha_now
        rho_bar = -cosine * alpha_now
        phi_value = cosine * phi_bar
        phi_bar = sine_value * phi_bar
        solution = solution + phi_value / rho_value * direction
        direction = model_unit - theta_value / rho_value * direction
    return (solution, direction)


def solution(mesh):
    return jax.shard_map(
        on_device,
        mesh=mesh,
        in_specs=(P("freq", None, "row", None),),
        out_specs=(P("freq", None, "row", None), P("freq", None, "row", None)),
        check_vma=False,
    )
```

profile of v0, /device:TPU:12, one launch (start us, length us, event | category | flops | bytes accessed | tf_op | source)
XLA Modules:
  0.0 439.7 jit_solution(2059661497259600702)
XLA Ops:
  7.2 0.0 all-gather.2.cloned.1.call-start
  7.2 0.7 all-gather.2.cloned.1.call-update
  7.9 151.1 %all-gather.2.cloned.1.call-done = bf16[1,2,2048,2048]{3,2,1,0:T(8,128)(2,1)} async-done(((bf16[1,2,256,2048]{3,2,1,0:T(8,128)(2,1)}), bf16[1,2,2048,2048]{3,2,1,0:T(8,128)(2,1)}) %all-gather.2.cloned.1.call-update) | async-done | bytes 16777232 | tf_op jit(solution)/shard_map/all_gather | solution.py:34
  159.1 6.2 %fusion.20 = f32[256,2048]{1,0:T(8,128)S(1)} fusion(bf16[1,2,256,2048]{3,2,1,0:T(8,128)(2,1)} %param.1, bf16[1,2,2048,2048]{3,2,1,0:T(8,128)(2,1)} %all-gather.2.cloned.1.call-done), kind=kOutput, calls=%fused_computation.65 | convolution fusion | flops 2147483648 | bytes 11534336 | tf_op jit(solution)/shard_map/frk,fnk->frn/dot_general | solution.py:23
  165.3 0.0 slice-start.2
  165.3 0.0 slice-start.3
  165.3 5.9 %fusion.24 = f32[256,2048]{1,0:T(8,128)S(1)} fusion(bf16[1,2,256,2048]{3,2,1,0:T(8,128)(2,1)S(1)} %copy-done.3, bf16[1,2,2048,2048]{3,2,1,0:T(8,128)(2,1)} %all-gather.2.cloned.1.call-done), kind=kOutput, calls=%fused_computation.69 | convolution fusion | flops 2147483648 | bytes 11534336 | tf_op jit(solution)/shard_map/frk,fnk->frn/dot_general | solution.py:20
  171.2 2.4 fusion.18
  173.6 0.0 copy-start.5
  173.6 2.4 fusion.19
  176.0 0.0 copy-start.7
  176.0 1.9 multiply_reduce_fusion.8
  178.0 44.0 %all-reduce.2 = (f32[]{:T(128)}, f32[]{:T(128)}, f32[]{:T(128)}, f32[]{:T(128)}) all-reduce(f32[]{:T(128)} %get-tuple-element.7, f32[]{:T(128)} %get-tuple-element.12, f32[]{:T(128)} %get-tuple-element.6, f32[]{:T(128)} %constant.2.clone.1), channel_id=1, replica_groups=mesh['freq'=4,'row'=8] {'freq','row'}, use_global_device_ids=true, to_apply=%region_1.0 | all-reduce | flops 4 | bytes 32 | tf_op jit(solution)/shard_map/psum | solution.py:38
  224.6 4.4 %fusion.38 = bf16[1,2,256,2048]{3,2,1,0:T(8,128)(2,1)} fusion(f32[]{:T(128)S(6)} %mul.197, f32[]{:T(128)S(6)} %sqrt.24, f32[1,1,256,2048]{3,2,1,0:T(8,128)} %copy-done.5, f32[1,1,256,2048]{3,2,1,0:T(8,128)} %copy-done.7, bf16[1,2,256,2048]{3,2,1,0:T(8,128)(2,1)S(1)} %copy-done.3), kind=kLoop, calls=%fused_computation.83 | loop fusion | flops 7340032 | bytes 8388616 | tf_op jit(solution)/shard_map/convert_element_type | solution.py:61
  229.0 6.2 %fusion.26 = f32[256,2048]{1,0:T(8,128)S(1)} fusion(bf16[1,2,256,2048]{3,2,1,0:T(8,128)(2,1)} %fusion.38, bf16[1,2,2048,2048]{3,2,1,0:T(8,128)(2,1)} %all-gather.2.cloned.1.call-done), kind=kOutput, calls=%fused_computation.71 | convolution fusion | flops 2147483648 | bytes 11534336 | tf_op jit(solution)/shard_map/frk,fkn->frn/dot_general | solution.py:13
  235.2 5.7 %fusion.27 = f32[256,2048]{1,0:T(8,128)S(1)} fusion(bf16[1,2,256,2048]{3,2,1,0:T(8,128)(2,1)S(1)} %copy-done.12, bf16[1,2,2048,2048]{3,2,1,0:T(8,128)(2,1)} %all-gather.2.cloned.1.call-done), kind=kOutput, calls=%fused_computation.72 | convolution fusion | flops 2147483648 | bytes 11534336 | tf_op jit(solution)/shard_map/frk,fkn->frn/dot_general | solution.py:10
  240.9 5.8 %fusion.16 = f32[1,1,256,2048]{3,2,1,0:T(8,128)S(1)} fusion(f32[256,2048]{1,0:T(8,128)S(1)} %fusion.26, bf16[1,2,256,2048]{3,2,1,0:T(8,128)(2,1)S(1)} %copy-done.12, bf16[1,2,2048,2048]{3,2,1,0:T(8,128)(2,1)} %all-gather.2.cloned.1.call-done), kind=kOutput, calls=%fused_computation.48 | convolution fusion | flops 2148007936 | bytes 13631488 | tf_op jit(solution)/shard_map/frk,fkn->frn/dot_general | solution.py:15
  246.7 0.0 copy-start.6
  246.7 0.0 copy-start.8
  246.7 5.9 %fusion.17 = f32[1,1,256,2048]{3,2,1,0:T(8,128)S(1)} fusion(f32[256,2048]{1,0:T(8,128)S(1)} %fusion.27, bf16[1,2,256,2048]{3,2,1,0:T(8,128)(2,1)S(1)} %copy-done.12, bf16[1,2,2048,2048]{3,2,1,0:T(8,128)(2,1)} %all-gather.2.cloned.1.call-done), kind=kOutput, calls=%fused_computation.50 | convolution fusion | flops 2148007936 | bytes 13631488 | tf_op jit(solution)/shard_map/frk,fkn->frn/dot_general | solution.py:12
  252.7 1.9 fusion.42
  254.6 0.0 copy-start
  254.6 7.3 %fusion.29 = f32[256,2048]{1,0:T(8,128)S(1)} fusion(bf16[1,2,256,2048]{3,2,1,0:T(8,128)(2,1)S(1)} %get-tuple-element.30, bf16[1,2,2048,2048]{3,2,1,0:T(8,128)(2,1)} %all-gather.2.cloned.1.call-done), kind=kOutput, calls=%fused_computation.74 | convolution fusion | flops 2147483648 | bytes 11534336 | tf_op jit(solution)/shard_map/frk,fnk->frn/dot_general | solution.py:23
  261.9 5.7 %fusion.28 = f32[256,2048]{1,0:T(8,128)S(1)} fusion(bf16[1,2,256,2048]{3,2,1,0:T(8,128)(2,1)S(1)} %get-tuple-element.30, bf16[1,2,2048,2048]{3,2,1,0:T(8,128)(2,1)} %all-gather.2.cloned.1.call-done), kind=kOutput, calls=%fused_computation.73 | convolution fusion | flops 2147483648 | bytes 11534336 | tf_op jit(solution)/shard_map/frk,fnk->frn/dot_general | solution.py:20
  267.6 5.7 %fusion.14 = f32[1,1,256,2048]{3,2,1,0:T(8,128)S(1)} fusion(f32[256,2048]{1,0:T(8,128)S(1)} %fusion.29, bf16[1,2,256,2048]{3,2,1,0:T(8,128)(2,1)S(1)} %get-tuple-element.30, bf16[1,2,2048,2048]{3,2,1,0:T(8,128)(2,1)} %all-gather.2.cloned.1.call-done), kind=kOutput, calls=%fused_computation.44 | convolution fusion | flops 2148007936 | bytes 13631488 | tf_op jit(solution)/shard_map/frk,fnk->frn/dot_general | solution.py:25
  273.4 6.5 %fusion.15 = f32[1,1,256,2048]{3,2,1,0:T(8,128)S(1)} fusion(f32[256,2048]{1,0:T(8,128)S(1)} %fusion.28, bf16[1,2,256,2048]{3,2,1,0:T(8,128)(2,1)S(1)} %get-tuple-element.30, bf16[1,2,2048,2048]{3,2,1,0:T(8,128)(2,1)} %all-gather.2.cloned.1.call-done), kind=kOutput, calls=%fused_computation.46 | convolution fusion | flops 2148007936 | bytes 13631488 | tf_op jit(solution)/shard_map/frk,fnk->frn/dot_general | solution.py:22
  279.9 0.0 copy-start.11
  279.9 4.2 multiply_reduce_fusion.5
  284.1 39.4 %all-reduce.1 = (f32[]{:T(128)}, f32[]{:T(128)}, f32[]{:T(128)}, f32[]{:T(128)}) all-reduce(f32[]{:T(128)} %get-tuple-element.11, f32[]{:T(128)} %get-tuple-element.5, f32[]{:T(128)} %get-tuple-element.4, f32[]{:T(128)} %get-tuple-element.10), channel_id=1, replica_groups=mesh['freq'=4,'row'=8] {'freq','row'}, use_global_device_ids=true, to_apply=%region_8.0 | all-reduce | flops 4 | bytes 32 | tf_op jit(solution)/shard_map/psum | solution.py:38
  326.2 0.0 slice-start.4
  326.2 0.0 slice-start.5
  326.2 0.0 slice-start.6
  326.2 5.5 %fusion.41 = (bf16[1,2,256,2048]{3,2,1,0:T(8,128)(2,1)S(1)}, f32[1,2,256,2048]{3,2,1,0:T(8,128)S(1)}) fusion(f32[1,2,256,2048]{3,2,1,0:T(8,128)} %get-tuple-element.29, f32[]{:T(128)S(6)} %sqrt.26, f32[1,2,256,2048]{3,2,1,0:T(8,128)} %copy-done, f32[1,1,256,2048]{3,2,1,0:T(8,128)} %copy-done.10, f32[1,1,256,2048]{3,2,1,0:T(8,128)} %copy-done.11), kind=kLoop, calls=%fused_computation.85 | loop fusion | flops 7340032 | bytes 18874372 | tf_op jit(solution)/shard_map/convert_element_type | solution.py:61
  331.7 0.0 slice-start.7
  331.7 8.1 %fusion.30 = f32[256,2048]{1,0:T(8,128)S(1)} fusion(bf16[1,2,256,2048]{3,2,1,0:T(8,128)(2,1)S(1)} %get-tuple-element.27, bf16[1,2,2048,2048]{3,2,1,0:T(8,128)(2,1)} %all-gather.2.cloned.1.call-done), kind=kOutput, calls=%fused_computation.75 | convolution fusion | flops 2147483648 | bytes 11534336 | tf_op jit(solution)/shard_map/frk,fkn->frn/dot_general | solution.py:13
  339.8 2.3 fusion.31
  342.2 2.4 fusion.12
  344.6 0.0 copy-start.1
  344.6 5.9 %fusion.13 = f32[1,1,256,2048]{3,2,1,0:T(8,128)S(1)} fusion(f32[256,2048]{1,0:T(8,128)S(1)} %fusion.31, bf16[1,2,256,2048]{3,2,1,0:T(8,128)(2,1)S(1)} %get-tuple-element.27, bf16[1,2,2048,2048]{3,2,1,0:T(8,128)(2,1)} %all-gather.2.cloned.1.call-done), kind=kOutput, calls=%fused_computation.42 | convolution fusion | flops 2148007936 | bytes 13631488 | tf_op jit(solution)/shard_map/frk,fkn->frn/dot_general | solution.py:12
  350.5 1.6 fusion.39
  352.1 0.0 copy-start.4
  352.1 7.3 %fusion.33 = f32[256,2048]{1,0:T(8,128)S(1)} fusion(bf16[1,2,256,2048]{3,2,1,0:T(8,128)(2,1)S(1)} %get-tuple-element.25, bf16[1,2,2048,2048]{3,2,1,0:T(8,128)(2,1)} %all-gather.2.cloned.1.call-done), kind=kOutput, calls=%fused_computation.78 | convolution fusion | flops 2147483648 | bytes 11534336 | tf_op jit(solution)/shard_map/frk,fnk->frn/dot_general | solution.py:23
  359.4 5.7 %fusion.32 = f32[256,2048]{1,0:T(8,128)S(1)} fusion(bf16[1,2,256,2048]{3,2,1,0:T(8,128)(2,1)S(1)} %get-tuple-element.25, bf16[1,2,2048,2048]{3,2,1,0:T(8,128)(2,1)} %all-gather.2.cloned.1.call-done), kind=kOutput, calls=%fused_computation.77 | convolution fusion | flops 2147483648 | bytes 11534336 | tf_op jit(solution)/shard_map/frk,fnk->frn/dot_general | solution.py:20
  365.2 5.7 %fusion.10 = f32[1,1,256,2048]{3,2,1,0:T(8,128)S(1)} fusion(f32[256,2048]{1,0:T(8,128)S(1)} %fusion.33, bf16[1,2,256,2048]{3,2,1,0:T(8,128)(2,1)S(1)} %get-tuple-element.25, bf16[1,2,2048,2048]{3,2,1,0:T(8,128)(2,1)} %all-gather.2.cloned.1.call-done), kind=kOutput, calls=%fused_computation.36 | convolution fusion | flops 2148007936 | bytes 13631488 | tf_op jit(solution)/shard_map/frk,fnk->frn/dot_general | solution.py:25
  370.9 5.7 %fusion.11 = f32[1,1,256,2048]{3,2,1,0:T(8,128)S(1)} fusion(f32[256,2048]{1,0:T(8,128)S(1)} %fusion.32, bf16[1,2,256,2048]{3,2,1,0:T(8,128)(2,1)S(1)} %get-tuple-element.25, bf16[1,2,2048,2048]{3,2,1,0:T(8,128)(2,1)} %all-gather.2.cloned.1.call-done), kind=kOutput, calls=%fused_computation.38 | convolution fusion | flops 2148007936 | bytes 13631488 | tf_op jit(solution)/shard_map/frk,fnk->frn/dot_general | solution.py:22
  376.7 2.2 multiply_reduce_fusion.1
  378.9 42.1 %all-reduce = (f32[]{:T(128)}, f32[]{:T(128)}, f32[]{:T(128)}, f32[]{:T(128)}) all-reduce(f32[]{:T(128)} %get-tuple-element.9, f32[]{:T(128)} %get-tuple-element.3, f32[]{:T(128)} %get-tuple-element.2, f32[]{:T(128)} %get-tuple-element.8), channel_id=1, replica_groups=mesh['freq'=4,'row'=8] {'freq','row'}, use_global_device_ids=true, to_apply=%region_16.0 | all-reduce | flops 4 | bytes 32 | tf_op jit(solution)/shard_map/psum | solution.py:38
  424.0 8.7 %multiply_subtract_fusion = (f32[1,2,256,2048]{3,2,1,0:T(8,128)}, f32[1,2,256,2048]{3,2,1,0:T(8,128)}) fusion(f32[1,2,256,2048]{3,2,1,0:T(8,128)} %get-tuple-element.29, f32[]{:T(128)S(6)} %div.111, f32[]{:T(128)S(6)} %sqrt.31, f32[]{:T(128)S(6)} %sqrt.29, f32[]{:T(128)S(6)} %div.104, f32[1,2,256,2048]{3,2,1,0:T(8,128)} %copy-done.4, ...), kind=kLoop, calls=%fused_computation.20 | loop fusion | flops 15728640 | bytes 25165852 | tf_op jit(solution)/shard_map/sub | solution.py:76
  (30 shorter events, 0.1 us)
Async XLA Ops:
  7.2 151.9 %all-gather.2.cloned.1.call-start = ((), (), s32[]{:S(2)}) async-start(), calls=%async_computation | async-start | bytes 18874368 | tf_op jit(solution)/shard_map/all_gather | solution.py:34
  7.9 157.4 %copy-start.3 = (bf16[1,2,256,2048]{3,2,1,0:T(8,128)(2,1)S(1)}, bf16[1,2,256,2048]{3,2,1,0:T(8,128)(2,1)}, u32[]{:S(2)}) copy-start(bf16[1,2,256,2048]{3,2,1,0:T(8,128)(2,1)} %param.1) | copy-start | bytes 6291460
  159.1 12.1 %slice-start = ((s8[16777216]{0:T(1024)(128)(4,1)}), s8[4194304]{0:T(1024)(128)(4,1)S(1)}, s32[]{:S(2)}) async-start(s8[16777216]{0:T(1024)(128)(4,1)} %bitcast.86), calls=%async_computation.1 | async-start | bytes 8388608
  159.1 12.2 %slice-start.1 = ((s8[16777216]{0:T(1024)(128)(4,1)}), s8[4194304]{0:T(1024)(128)(4,1)S(1)}, s32[]{:S(2)}) async-start(s8[16777216]{0:T(1024)(128)(4,1)} %bitcast.86), calls=%async_computation.2 | async-start | bytes 8388608
  165.3 5.9 %slice-start.2 = ((s8[16777216]{0:T(1024)(128)(4,1)}), s8[4194304]{0:T(1024)(128)(4,1)S(1)}, s32[]{:S(2)}) async-start(s8[16777216]{0:T(1024)(128)(4,1)} %bitcast.86), calls=%async_computation.3 | async-start | bytes 8388608
  165.3 5.9 %slice-start.3 = ((s8[16777216]{0:T(1024)(128)(4,1)}), s8[4194304]{0:T(1024)(128)(4,1)S(1)}, s32[]{:S(2)}) async-start(s8[16777216]{0:T(1024)(128)(4,1)} %bitcast.86), calls=%async_computation.4 | async-start | bytes 8388608
  173.6 2.4 copy-start.5
  176.0 1.9 copy-start.7
  229.0 6.2 %copy-start.12 = (bf16[1,2,256,2048]{3,2,1,0:T(8,128)(2,1)S(1)}, bf16[1,2,256,2048]{3,2,1,0:T(8,128)(2,1)}, u32[]{:S(2)}) copy-start(bf16[1,2,256,2048]{3,2,1,0:T(8,128)(2,1)} %fusion.38) | copy-start | bytes 6291460
  246.7 6.0 %copy-start.6 = (f32[1,1,256,2048]{3,2,1,0:T(8,128)S(1)}, f32[1,1,256,2048]{3,2,1,0:T(8,128)}, u32[]{:S(2)}) copy-start(f32[1,1,256,2048]{3,2,1,0:T(8,128)} %copy-done.5) | copy-start | bytes 6291460
  246.7 6.0 %copy-start.8 = (f32[1,1,256,2048]{3,2,1,0:T(8,128)S(1)}, f32[1,1,256,2048]{3,2,1,0:T(8,128)}, u32[]{:S(2)}) copy-start(f32[1,1,256,2048]{3,2,1,0:T(8,128)} %copy-done.7) | copy-start | bytes 6291460
  254.6 25.3 %copy-start = (f32[1,2,256,2048]{3,2,1,0:T(8,128)}, f32[1,2,256,2048]{3,2,1,0:T(8,128)S(1)}, u32[]{:S(2)}) copy-start(f32[1,2,256,2048]{3,2,1,0:T(8,128)S(1)} %get-tuple-element.31) | copy-start | bytes 12582916
  273.4 6.5 %copy-start.10 = (f32[1,1,256,2048]{3,2,1,0:T(8,128)}, f32[1,1,256,2048]{3,2,1,0:T(8,128)S(1)}, u32[]{:S(2)}) copy-start(f32[1,1,256,2048]{3,2,1,0:T(8,128)S(1)} %fusion.14) | copy-start | bytes 6291460
  279.9 4.3 copy-start.11
  326.2 13.6 %slice-start.4 = ((s8[16777216]{0:T(1024)(128)(4,1)}), s8[4194304]{0:T(1024)(128)(4,1)S(1)}, s32[]{:S(2)}) async-start(s8[16777216]{0:T(1024)(128)(4,1)} %bitcast.88), calls=%async_computation.5 | async-start | bytes 8388608
  326.2 13.6 %slice-start.5 = ((s8[16777216]{0:T(1024)(128)(4,1)}), s8[4194304]{0:T(1024)(128)(4,1)S(1)}, s32[]{:S(2)}) async-start(s8[16777216]{0:T(1024)(128)(4,1)} %bitcast.88), calls=%async_computation.6 | async-start | bytes 8388608
  326.2 13.6 %slice-start.6 = ((s8[16777216]{0:T(1024)(128)(4,1)}), s8[4194304]{0:T(1024)(128)(4,1)S(1)}, s32[]{:S(2)}) async-start(s8[16777216]{0:T(1024)(128)(4,1)} %bitcast.88), calls=%async_computation.7 | async-start | bytes 8388608
  331.7 45.0 %copy-start.2 = (f32[1,2,256,2048]{3,2,1,0:T(8,128)}, f32[1,2,256,2048]{3,2,1,0:T(8,128)S(1)}, u32[]{:S(2)}) copy-start(f32[1,2,256,2048]{3,2,1,0:T(8,128)S(1)} %get-tuple-element.28) | copy-start | bytes 12582916
  331.7 8.1 %slice-start.7 = ((s8[16777216]{0:T(1024)(128)(4,1)}), s8[4194304]{0:T(1024)(128)(4,1)S(1)}, s32[]{:S(2)}) async-start(s8[16777216]{0:T(1024)(128)(4,1)} %bitcast.88), calls=%async_computation.8 | async-start | bytes 8388608
  344.6 5.9 %copy-start.1 = (f32[1,2,256,2048]{3,2,1,0:T(8,128)S(1)}, f32[1,2,256,2048]{3,2,1,0:T(8,128)}, u32[]{:S(2)}) copy-start(f32[1,2,256,2048]{3,2,1,0:T(8,128)} %copy-done) | copy-start | bytes 12582916
  352.1 24.5 %copy-start.4 = (f32[1,2,256,2048]{3,2,1,0:T(8,128)}, f32[1,2,256,2048]{3,2,1,0:T(8,128)S(1)}, u32[]{:S(2)}) copy-start(f32[1,2,256,2048]{3,2,1,0:T(8,128)S(1)} %get-tuple-element.26) | copy-start | bytes 12582916
  376.7 2.2 copy-start.9
Sparse Core Ops, SparseCore 0:
  9.6 149.4 all-gather.1
where the time goes:
time: 447 us; the launch traced here: 440 us
  waiting for transfers between devices  152 us (34%)
  blocking collectives  126 us (28%)
  matrix products  109 us (24%)
  other arithmetic  30.5 us (7%)
  between operations  22.8 us (5%)
    all_gather x1, waiting for transfers between devices, on_device(): whole = lax.all_gather(data, 'row', axis=2, tiled=True)  151 us
    psum x3, blocking collectives, pair_step(): lax.psum((jnp.sum(data_raw * data_raw), jnp.sum(image * image), jnp.sum(i...  126 us
    dot_general x3, matrix products, times_adjoint(): jnp.einsum('frk,fnk->frn', rounded[:, 1], block[:, 0], preferred_element_...  20.7 us
    dot_general x3, matrix products, times_adjoint(): jnp.einsum('frk,fnk->frn', rounded[:, 0], block[:, 0], preferred_element_...  17.4 us
    dot_general x3, matrix products, times_adjoint(): jnp.einsum('frk,fnk->frn', rounded[:, 1], block[:, 1], preferred_element_...  14.6 us
    dot_general x2, matrix products, times_data(): jnp.einsum('frk,fkn->frn', rounded[:, 0], block[:, 1], preferred_element_...  14.2 us
    dot_general x3, matrix products, times_adjoint(): jnp.einsum('frk,fnk->frn', rounded[:, 0], block[:, 1], preferred_element_...  13.9 us
    dot_general x2, matrix products, times_data(): jnp.einsum('frk,fkn->frn', rounded[:, 1], block[:, 1], preferred_element_...  11.8 us
  transfers between devices with their start and end apart: 1, of which 1 were waited for; matrix products, arithmetic and copies ran while one was open for 0% of the time, Pallas kernels for 0%

commit v1 on v0

--- a/solution.py
+++ b/solution.py
@@ -31,7 +31,12 @@
     weight = 1.0 / (3.0 * (2.0 * order) ** 0.5)
     observed = data.astype(jnp.float32)
     zeros = jnp.zeros_like(observed)
-    whole = lax.all_gather(data, "row", axis=2, tiled=True)
+    ring = [data]
+    for hop in range(7):
+        ring.append(lax.ppermute(ring[-1], "row", [(dev, (dev + 1) % 8) for dev in range(8)]))
+    whole = jnp.roll(
+        jnp.concatenate(ring[::-1], axis=2), (lax.axis_index("row") + 1) * ring[0].shape[2], axis=2
+    )
     first_image = observed - weight * times_adjoint(observed.astype(jnp.bfloat16), whole)
 
     def pair_step(data_raw, model_unit, image):

time: 447 us -> 555 us (1.24)
  local copies, waits for them, and re-layouts: 0.1 us -> 51.8 us
  matrix products: 109 us -> 141 us
  waiting for transfers between devices: 152 us -> 176 us
  between operations: 22.8 us -> 9.72 us
  blocking collectives: 126 us -> 135 us
    ppermute x0 -> x7, waiting for transfers between devices: none -> 176 us  [on_device(): lax.ppermute(ring[-1], 'row', [(dev, (dev + 1) % 8) for dev in range(8)])]
    all_gather x1 -> x0, waiting for transfers between devices: 151 us -> none  [on_device(): whole = lax.all_gather(data, 'row', axis=2, tiled=True)]
    unnamed x42 -> x78, local copies, waits for them, and re-layouts: 0.1 us -> 50.3 us
    psum x3, blocking collectives: 126 us -> 135 us  [pair_step(): lax.psum((jnp.sum(data_raw * data_raw), jnp.sum(image * image), jnp.sum(i...]
    dot_general x2, matrix products: 8.19 us -> 16.9 us  [times_data(): jnp.einsum('frk,fkn->frn', rounded[:, 1], block[:, 0], preferred_element_...]
    dot_general x3, matrix products: 13.9 us -> 21 us  [times_adjoint(): jnp.einsum('frk,fnk->frn', rounded[:, 0], block[:, 1], preferred_element_...]
    dot_general x2, matrix products: 8.06 us -> 14.5 us  [times_data(): jnp.einsum('frk,fkn->frn', rounded[:, 0], block[:, 0], preferred_element_...]
  transfers between devices with their start and end apart: 1 -> 7, of which waited for: 1 -> 7; matrix products, arithmetic and copies ran while one was open for 0% -> 1% of each run, Pallas kernels for 0% -> 0%
where the time goes in v1:
time: 555 us; the launch traced here: 545 us
  waiting for transfers between devices  176 us (32%)
  matrix products  141 us (25%)
  blocking collectives  135 us (24%)
  local copies, waits for them, and re-layouts  51.8 us (9%)
  other arithmetic  32 us (6%)
  between operations  9.72 us (2%)
    ppermute x7, waiting for transfers between devices, on_device(): lax.ppermute(ring[-1], 'row', [(dev, (dev + 1) % 8) for dev in range(8)])  176 us
    psum x3, blocking collectives, pair_step(): lax.psum((jnp.sum(data_raw * data_raw), jnp.sum(image * image), jnp.sum(i...  135 us
    unnamed x78, local copies, waits for them, and re-layouts  50.3 us
    dot_general x3, matrix products, times_adjoint(): jnp.einsum('frk,fnk->frn', rounded[:, 0], block[:, 1], preferred_element_...  21 us
    dot_general x3, matrix products, times_adjoint(): jnp.einsum('frk,fnk->frn', rounded[:, 0], block[:, 0], preferred_element_...  19.4 us
    dot_general x3, matrix products, times_adjoint(): jnp.einsum('frk,fnk->frn', rounded[:, 1], block[:, 0], preferred_element_...  18.7 us
    dot_general x3, matrix products, times_adjoint(): jnp.einsum('frk,fnk->frn', rounded[:, 1], block[:, 1], preferred_element_...  18.7 us
    dot_general x2, matrix products, times_data(): jnp.einsum('frk,fkn->frn', rounded[:, 1], block[:, 0], preferred_element_...  16.9 us
  transfers between devices with their start and end apart: 7, of which 7 were waited for; matrix products, arithmetic and copies ran while one was open for 1% of the time, Pallas kernels for 0%

profile of v1, /device:TPU:12, one launch (start us, length us, event | category | flops | bytes accessed | tf_op | source)
XLA Modules:
  0.0 544.6 jit_solution(952164531706060128)
XLA Ops:
  0.7 25.7 %collective-permute-done = bf16[1,2,256,2048]{3,2,1,0:T(8,128)(2,1)S(1)} collective-permute-done((bf16[1,2,256,2048]{3,2,1,0:T(8,128)(2,1)}, bf16[1,2,256,2048]{3,2,1,0:T(8,128)(2,1)S(1)}, u32[]{:S(2)}, u32[]{:S(2)}) %collective-permute-start) | collective-permute-done | bytes 2097184 | tf_op jit(solution)/shard_map/ppermute | solution.py:36
  27.7 25.5 %collective-permute-done.1 = bf16[1,2,256,2048]{3,2,1,0:T(8,128)(2,1)S(1)} collective-permute-done((bf16[1,2,256,2048]{3,2,1,0:T(8,128)(2,1)S(1)}, bf16[1,2,256,2048]{3,2,1,0:T(8,128)(2,1)S(1)}, u32[]{:S(2)}, u32[]{:S(2)}) %collective-permute-start.1) | collective-permute-done | bytes 2097184 | tf_op jit(solution)/shard_map/ppermute | solution.py:36
  54.4 25.5 %collective-permute-done.2 = bf16[1,2,256,2048]{3,2,1,0:T(8,128)(2,1)S(1)} collective-permute-done((bf16[1,2,256,2048]{3,2,1,0:T(8,128)(2,1)S(1)}, bf16[1,2,256,2048]{3,2,1,0:T(8,128)(2,1)S(1)}, u32[]{:S(2)}, u32[]{:S(2)}) %collective-permute-start.2) | collective-permute-done | bytes 2097184 | tf_op jit(solution)/shard_map/ppermute | solution.py:36
  81.2 25.5 %collective-permute-done.3 = bf16[1,2,256,2048]{3,2,1,0:T(8,128)(2,1)S(1)} collective-permute-done((bf16[1,2,256,2048]{3,2,1,0:T(8,128)(2,1)S(1)}, bf16[1,2,256,2048]{3,2,1,0:T(8,128)(2,1)S(1)}, u32[]{:S(2)}, u32[]{:S(2)}) %collective-permute-start.3) | collective-permute-done | bytes 2097184 | tf_op jit(solution)/shard_map/ppermute | solution.py:36
  108.0 25.5 %collective-permute-done.4 = bf16[1,2,256,2048]{3,2,1,0:T(8,128)(2,1)S(1)} collective-permute-done((bf16[1,2,256,2048]{3,2,1,0:T(8,128)(2,1)S(1)}, bf16[1,2,256,2048]{3,2,1,0:T(8,128)(2,1)S(1)}, u32[]{:S(2)}, u32[]{:S(2)}) %collective-permute-start.4) | collective-permute-done | bytes 2097184 | tf_op jit(solution)/shard_map/ppermute | solution.py:36
  134.8 25.6 %collective-permute-done.5 = bf16[1,2,256,2048]{3,2,1,0:T(8,128)(2,1)} collective-permute-done((bf16[1,2,256,2048]{3,2,1,0:T(8,128)(2,1)S(1)}, bf16[1,2,256,2048]{3,2,1,0:T(8,128)(2,1)}, u32[]{:S(2)}, u32[]{:S(2)}) %collective-permute-start.5) | collective-permute-done | bytes 2097184 | tf_op jit(solution)/shard_map/ppermute | solution.py:36
  160.4 2.8 copy.3
  163.2 22.9 %collective-permute-done.6 = bf16[1,2,256,2048]{3,2,1,0:T(8,128)(2,1)} collective-permute-done((bf16[1,2,256,2048]{3,2,1,0:T(8,128)(2,1)}, bf16[1,2,256,2048]{3,2,1,0:T(8,128)(2,1)}, u32[]{:S(2)}, u32[]{:S(2)}) %collective-permute-start.6) | collective-permute-done | bytes 2097184 | tf_op jit(solution)/shard_map/ppermute | solution.py:36
  186.1 3.2 constant_dynamic-update-slice_fusion.15
  189.3 3.5 constant_dynamic-update-slice_fusion.14
  197.4 1.6 constant_dynamic-update-slice_fusion.10
  200.5 1.5 constant_dynamic-update-slice_fusion.8
  202.0 3.3 constant_dynamic-update-slice_fusion.7
  205.3 3.2 constant_dynamic-update-slice_fusion.6
  211.5 1.6 constant_dynamic-update-slice_fusion.3
  217.7 5.9 %fusion.23 = f32[2048,256]{1,0:T(8,128)S(1)} fusion(bf16[1,2,256,2048]{3,2,1,0:T(8,128)(2,1)S(1)} %copy-done.9, bf16[1,2,4096,2048]{3,2,1,0:T(8,128)(2,1)} %constant_dynamic-update-slice_fusion, s32[]{:T(128)S(6)} %add.94, s32[]{:T(128)S(6)} %select_n.14), kind=kOutput, calls=%fused_computation.68 | convolution fusion | flops 2147483648 | bytes 11534344 | tf_op jit(solution)/shard_map/frk,fnk->frn/dot_general | solution.py:25
  223.6 5.9 %fusion.21 = f32[2048,256]{1,0:T(8,128)S(1)} fusion(bf16[1,2,256,2048]{3,2,1,0:T(8,128)(2,1)S(1)} %copy-done.9, bf16[1,2,4096,2048]{3,2,1,0:T(8,128)(2,1)} %constant_dynamic-update-slice_fusion, s32[]{:T(128)S(6)} %add.94, s32[]{:T(128)S(6)} %select_n.14), kind=kOutput, calls=%fused_computation.66 | convolution fusion | flops 2147483648 | bytes 11534344 | tf_op jit(solution)/shard_map/frk,fnk->frn/dot_general | solution.py:22
  229.5 6.0 %fusion.18 = f32[1,1,256,2048]{2,3,1,0:T(8,128)S(1)} fusion(f32[2048,256]{1,0:T(8,128)S(1)} %fusion.23, bf16[1,2,256,2048]{3,2,1,0:T(8,128)(2,1)S(1)} %copy-done.9, bf16[1,2,4096,2048]{3,2,1,0:T(8,128)(2,1)} %constant_dynamic-update-slice_fusion, s32[]{:T(128)S(6)} %select_n.14), kind=kOutput, calls=%fused_computation.52 | convolution fusion | flops 2148007936 | bytes 13631492 | tf_op jit(solution)/shard_map/frk,fnk->frn/dot_general | solution.py:23
  235.5 6.8 %fusion.19 = f32[1,1,256,2048]{2,3,1,0:T(8,128)S(1)} fusion(f32[2048,256]{1,0:T(8,128)S(1)} %fusion.21, bf16[1,2,256,2048]{3,2,1,0:T(8,128)(2,1)S(1)} %copy-done.9, bf16[1,2,4096,2048]{3,2,1,0:T(8,128)(2,1)} %constant_dynamic-update-slice_fusion, s32[]{:T(128)S(6)} %select_n.14), kind=kOutput, calls=%fused_computation.54 | convolution fusion | flops 2148007936 | bytes 13631492 | tf_op jit(solution)/shard_map/frk,fnk->frn/dot_general | solution.py:20
  242.3 2.1 multiply_reduce_fusion.8
  244.4 53.5 %all-reduce.2 = (f32[]{:T(128)}, f32[]{:T(128)}, f32[]{:T(128)}, f32[]{:T(128)}) all-reduce(f32[]{:T(128)} %get-tuple-element.9, f32[]{:T(128)} %get-tuple-element.14, f32[]{:T(128)} %get-tuple-element.8, f32[]{:T(128)} %constant.37.clone.1), channel_id=1, replica_groups=mesh['freq'=4,'row'=8] {'freq','row'}, use_global_device_ids=true, to_apply=%region_1.2 | all-reduce | flops 4 | bytes 32 | tf_op jit(solution)/shard_map/psum | solution.py:43
  298.7 3.0 fusion.38
  301.6 8.8 %fusion.26 = f32[256,2048]{0,1:T(8,128)} fusion(bf16[1,2,256,2048]{2,3,1,0:T(8,128)(2,1)S(1)} %fusion.38, bf16[1,2,4096,2048]{3,2,1,0:T(8,128)(2,1)} %constant_dynamic-update-slice_fusion, s32[]{:T(128)S(6)} %select_n.14), kind=kOutput, calls=%fused_computation.71 | convolution fusion | flops 2147483648 | bytes 11534340 | tf_op jit(solution)/shard_map/frk,fkn->frn/dot_general | solution.py:15
  310.5 8.1 %fusion.27 = f32[256,2048]{0,1:T(8,128)} fusion(bf16[1,2,256,2048]{2,3,1,0:T(8,128)(2,1)S(1)} %fusion.38, bf16[1,2,4096,2048]{3,2,1,0:T(8,128)(2,1)} %constant_dynamic-update-slice_fusion, s32[]{:T(128)S(6)} %add.94, s32[]{:T(128)S(6)} %select_n.14), kind=kOutput, calls=%fused_computation.72 | convolution fusion | flops 2147483648 | bytes 11534344 | tf_op jit(solution)/shard_map/frk,fkn->frn/dot_general | solution.py:12
  320.5 7.8 %fusion.16 = f32[1,1,256,2048]{2,3,1,0:T(8,128)S(1)} fusion(f32[256,2048]{0,1:T(8,128)} %fusion.26, bf16[1,2,256,2048]{2,3,1,0:T(8,128)(2,1)} %copy-done.25, bf16[1,2,4096,2048]{3,2,1,0:T(8,128)(2,1)} %constant_dynamic-update-slice_fusion, s32[]{:T(128)S(6)} %add.94, s32[]{:T(128)S(6)} %select_n.14), kind=kOutput, calls=%fused_computation.48 | convolution fusion | flops 2148007936 | bytes 13631496 | tf_op jit(solution)/shard_map/frk,fkn->frn/dot_general | solution.py:13
  328.3 7.3 %fusion.17 = f32[1,1,256,2048]{2,3,1,0:T(8,128)S(1)} fusion(f32[256,2048]{0,1:T(8,128)S(1)} %copy-done.27, bf16[1,2,256,2048]{2,3,1,0:T(8,128)(2,1)S(1)} %copy-done.26, bf16[1,2,4096,2048]{3,2,1,0:T(8,128)(2,1)} %constant_dynamic-update-slice_fusion, s32[]{:T(128)S(6)} %select_n.14), kind=kOutput, calls=%fused_computation.50 | convolution fusion | flops 2148007936 | bytes 13631492 | tf_op jit(solution)/shard_map/frk,fkn->frn/dot_general | solution.py:10
  335.7 1.7 fusion.42
  337.4 7.3 %fusion.28 = f32[256,2048]{0,1:T(8,128)S(1)} fusion(bf16[1,2,256,2048]{2,3,1,0:T(8,128)(2,1)S(1)} %get-tuple-element.32, bf16[1,2,4096,2048]{3,2,1,0:T(8,128)(2,1)} %constant_dynamic-update-slice_fusion, s32[]{:T(128)S(6)} %add.94, s32[]{:T(128)S(6)} %select_n.14), kind=kOutput, calls=%fused_computation.73 | convolution fusion | flops 2147483648 | bytes 11534344 | tf_op jit(solution)/shard_map/frk,fnk->frn/dot_general | solution.py:25
  344.6 5.7 %fusion.29 = f32[256,2048]{0,1:T(8,128)S(1)} fusion(bf16[1,2,256,2048]{2,3,1,0:T(8,128)(2,1)S(1)} %get-tuple-element.32, bf16[1,2,4096,2048]{3,2,1,0:T(8,128)(2,1)} %constant_dynamic-update-slice_fusion, s32[]{:T(128)S(6)} %add.94, s32[]{:T(128)S(6)} %select_n.14), kind=kOutput, calls=%fused_computation.74 | convolution fusion | flops 2147483648 | bytes 11534344 | tf_op jit(solution)/shard_map/frk,fnk->frn/dot_general | solution.py:22
  350.4 5.9 %fusion.12 = f32[1,1,256,2048]{2,3,1,0:T(8,128)S(1)} fusion(f32[256,2048]{0,1:T(8,128)S(1)} %fusion.28, bf16[1,2,256,2048]{2,3,1,0:T(8,128)(2,1)S(1)} %get-tuple-element.32, bf16[1,2,4096,2048]{3,2,1,0:T(8,128)(2,1)} %constant_dynamic-update-slice_fusion, s32[]{:T(128)S(6)} %select_n.14), kind=kOutput, calls=%fused_computation.40 | convolution fusion | flops 2148007936 | bytes 13631492 | tf_op jit(solution)/shard_map/frk,fnk->frn/dot_general | solution.py:23
  356.3 6.5 %fusion.13 = f32[1,1,256,2048]{2,3,1,0:T(8,128)S(1)} fusion(f32[256,2048]{0,1:T(8,128)S(1)} %fusion.29, bf16[1,2,256,2048]{2,3,1,0:T(8,128)(2,1)S(1)} %get-tuple-element.32, bf16[1,2,4096,2048]{3,2,1,0:T(8,128)(2,1)} %constant_dynamic-update-slice_fusion, s32[]{:T(128)S(6)} %select_n.14), kind=kOutput, calls=%fused_computation.42 | convolution fusion | flops 2148007936 | bytes 13631492 | tf_op jit(solution)/shard_map/frk,fnk->frn/dot_general | solution.py:20
  362.8 4.4 multiply_reduce_fusion.5
  367.2 38.9 %all-reduce.1 = (f32[]{:T(128)}, f32[]{:T(128)}, f32[]{:T(128)}, f32[]{:T(128)}) all-reduce(f32[]{:T(128)} %get-tuple-element.13, f32[]{:T(128)} %get-tuple-element.7, f32[]{:T(128)} %get-tuple-element.6, f32[]{:T(128)} %get-tuple-element.12), channel_id=1, replica_groups=mesh['freq'=4,'row'=8] {'freq','row'}, use_global_device_ids=true, to_apply=%region_8.9 | all-reduce | flops 4 | bytes 32 | tf_op jit(solution)/shard_map/psum | solution.py:43
  406.7 7.4 %fusion.41 = (bf16[1,2,256,2048]{2,3,1,0:T(8,128)(2,1)S(1)}, f32[1,2,256,2048]{2,3,1,0:T(8,128)}) fusion(f32[1,2,256,2048]{2,3,1,0:T(8,128)} %get-tuple-element.31, f32[]{:T(128)S(6)} %sqrt.26, f32[1,2,256,2048]{2,3,1,0:T(8,128)} %copy-done, f32[1,1,256,2048]{2,3,1,0:T(8,128)} %copy-done.21, f32[1,1,256,2048]{2,3,1,0:T(8,128)} %copy-done.22), kind=kLoop, calls=%fused_computation.101 | loop fusion | flops 7340032 | bytes 18874372 | tf_op jit(solution)/shard_map/convert_element_type | solution.py:66
  414.1 8.1 %fusion.30 = f32[256,2048]{0,1:T(8,128)} fusion(bf16[1,2,256,2048]{2,3,1,0:T(8,128)(2,1)S(1)} %get-tuple-element.29, bf16[1,2,4096,2048]{3,2,1,0:T(8,128)(2,1)} %constant_dynamic-update-slice_fusion, s32[]{:T(128)S(6)} %select_n.14), kind=kOutput, calls=%fused_computation.75 | convolution fusion | flops 2147483648 | bytes 11534340 | tf_op jit(solution)/shard_map/frk,fkn->frn/dot_general | solution.py:15
  422.2 8.1 %fusion.31 = f32[256,2048]{0,1:T(8,128)} fusion(bf16[1,2,256,2048]{2,3,1,0:T(8,128)(2,1)S(1)} %get-tuple-element.29, bf16[1,2,4096,2048]{3,2,1,0:T(8,128)(2,1)} %constant_dynamic-update-slice_fusion, s32[]{:T(128)S(6)} %add.94, s32[]{:T(128)S(6)} %select_n.14), kind=kOutput, calls=%fused_computation.76 | convolution fusion | flops 2147483648 | bytes 11534344 | tf_op jit(solution)/shard_map/frk,fkn->frn/dot_general | solution.py:12
  432.3 7.5 %fusion.14 = f32[1,1,256,2048]{2,3,1,0:T(8,128)S(1)} fusion(f32[256,2048]{0,1:T(8,128)} %fusion.30, bf16[1,2,256,2048]{2,3,1,0:T(8,128)(2,1)S(1)} %get-tuple-element.29, bf16[1,2,4096,2048]{3,2,1,0:T(8,128)(2,1)} %constant_dynamic-update-slice_fusion, s32[]{:T(128)S(6)} %add.94, s32[]{:T(128)S(6)} %select_n.14), kind=kOutput, calls=%fused_computation.44 | convolution fusion | flops 2148007936 | bytes 13631496 | tf_op jit(solution)/shard_map/frk,fkn->frn/dot_general | solution.py:13
  439.8 7.1 %fusion.15 = f32[1,1,256,2048]{2,3,1,0:T(8,128)S(1)} fusion(f32[256,2048]{0,1:T(8,128)S(1)} %copy-done.28, bf16[1,2,256,2048]{2,3,1,0:T(8,128)(2,1)S(1)} %get-tuple-element.29, bf16[1,2,4096,2048]{3,2,1,0:T(8,128)(2,1)} %constant_dynamic-update-slice_fusion, s32[]{:T(128)S(6)} %select_n.14), kind=kOutput, calls=%fused_computation.46 | convolution fusion | flops 2148007936 | bytes 13631492 | tf_op jit(solution)/shard_map/frk,fkn->frn/dot_general | solution.py:10
  447.0 2.5 fusion.39
  449.5 7.8 %fusion.32 = f32[256,2048]{0,1:T(8,128)} fusion(bf16[1,2,256,2048]{2,3,1,0:T(8,128)(2,1)S(1)} %get-tuple-element.27, bf16[1,2,4096,2048]{3,2,1,0:T(8,128)(2,1)} %constant_dynamic-update-slice_fusion, s32[]{:T(128)S(6)} %add.94, s32[]{:T(128)S(6)} %select_n.14), kind=kOutput, calls=%fused_computation.77 | convolution fusion | flops 2147483648 | bytes 11534344 | tf_op jit(solution)/shard_map/frk,fnk->frn/dot_general | solution.py:25
  457.3 7.1 %fusion.33 = f32[256,2048]{0,1:T(8,128)} fusion(bf16[1,2,256,2048]{2,3,1,0:T(8,128)(2,1)S(1)} %get-tuple-element.27, bf16[1,2,4096,2048]{3,2,1,0:T(8,128)(2,1)} %constant_dynamic-update-slice_fusion, s32[]{:T(128)S(6)} %add.94, s32[]{:T(128)S(6)} %select_n.14), kind=kOutput, calls=%fused_computation.78 | convolution fusion | flops 2147483648 | bytes 11534344 | tf_op jit(solution)/shard_map/frk,fnk->frn/dot_general | solution.py:22
  464.5 6.8 %fusion.10 = f32[1,1,256,2048]{2,3,1,0:T(8,128)S(1)} fusion(f32[256,2048]{0,1:T(8,128)} %fusion.32, bf16[1,2,256,2048]{2,3,1,0:T(8,128)(2,1)} %copy-done.23, bf16[1,2,4096,2048]{3,2,1,0:T(8,128)(2,1)} %constant_dynamic-update-slice_fusion, s32[]{:T(128)S(6)} %select_n.14), kind=kOutput, calls=%fused_computation.36 | convolution fusion | flops 2148007936 | bytes 13631492 | tf_op jit(solution)/shard_map/frk,fnk->frn/dot_general | solution.py:23
  471.4 6.1 %fusion.11 = f32[1,1,256,2048]{2,3,1,0:T(8,128)S(1)} fusion(f32[256,2048]{0,1:T(8,128)S(1)} %copy-done.29, bf16[1,2,256,2048]{2,3,1,0:T(8,128)(2,1)S(1)} %copy-done.24, bf16[1,2,4096,2048]{3,2,1,0:T(8,128)(2,1)} %constant_dynamic-update-slice_fusion, s32[]{:T(128)S(6)} %select_n.14), kind=kOutput, calls=%fused_computation.38 | convolution fusion | flops 2148007936 | bytes 13631492 | tf_op jit(solution)/shard_map/frk,fnk->frn/dot_general | solution.py:20
  477.5 2.5 multiply_reduce_fusion.1
  479.9 42.1 %all-reduce = (f32[]{:T(128)}, f32[]{:T(128)}, f32[]{:T(128)}, f32[]{:T(128)}) all-reduce(f32[]{:T(128)} %get-tuple-element.11, f32[]{:T(128)} %get-tuple-element.5, f32[]{:T(128)} %get-tuple-element.4, f32[]{:T(128)} %get-tuple-element.10), channel_id=1, replica_groups=mesh['freq'=4,'row'=8] {'freq','row'}, use_global_device_ids=true, to_apply=%region_16.17 | all-reduce | flops 4 | bytes 32 | tf_op jit(solution)/shard_map/psum | solution.py:43
  524.9 8.5 %multiply_subtract_fusion = (f32[1,2,256,2048]{2,3,1,0:T(8,128)}, f32[1,2,256,2048]{2,3,1,0:T(8,128)}) fusion(f32[1,2,256,2048]{2,3,1,0:T(8,128)} %get-tuple-element.31, f32[]{:T(128)S(6)} %div.111, f32[]{:T(128)S(6)} %sqrt.31, f32[]{:T(128)S(6)} %sqrt.29, f32[]{:T(128)S(6)} %div.104, f32[1,2,256,2048]{2,3,1,0:T(8,128)} %get-tuple-element.28, ...), kind=kLoop, calls=%fused_computation.20 | loop fusion | flops 15728640 | bytes 25165852 | tf_op jit(solution)/shard_map/sub | solution.py:81
  533.5 5.3 copy.20
  538.8 5.3 copy.21
  (76 shorter events, 20.4 us)
Async XLA Ops:
  0.6 25.7 %collective-permute-start = (bf16[1,2,256,2048]{3,2,1,0:T(8,128)(2,1)}, bf16[1,2,256,2048]{3,2,1,0:T(8,128)(2,1)S(1)}, u32[]{:S(2)}, u32[]{:S(2)}) collective-permute-start(bf16[1,2,256,2048]{3,2,1,0:T(8,128)(2,1)} %param.1), channel_id=1, source_target_pairs={{0,1},{1,2},{2,3},{3,4},{4,5},{5,6},{6,7},{7,0},{8,9},{9,10},{10,1... | collective-permute-start | bytes 6291464 | tf_op jit(solution)/shard_map/ppermute | solution.py:36
  26.4 1.3 copy-start.10
  27.7 25.5 %collective-permute-start.1 = (bf16[1,2,256,2048]{3,2,1,0:T(8,128)(2,1)S(1)}, bf16[1,2,256,2048]{3,2,1,0:T(8,128)(2,1)S(1)}, u32[]{:S(2)}, u32[]{:S(2)}) collective-permute-start(bf16[1,2,256,2048]{3,2,1,0:T(8,128)(2,1)S(1)} %collective-permute-done), channel_id=1, source_target_pairs={{0,1},{1,2},{2,3},{3,4},{4,5},{5,6},{6,7},{7,0},{8,9},{9,10},{10,1... | collective-permute-start | bytes 6291464 | tf_op jit(solution)/shard_map/ppermute | solution.py:36
  53.1 1.3 copy-start.12
  54.4 25.5 %collective-permute-start.2 = (bf16[1,2,256,2048]{3,2,1,0:T(8,128)(2,1)S(1)}, bf16[1,2,256,2048]{3,2,1,0:T(8,128)(2,1)S(1)}, u32[]{:S(2)}, u32[]{:S(2)}) collective-permute-start(bf16[1,2,256,2048]{3,2,1,0:T(8,128)(2,1)S(1)} %collective-permute-done.1), channel_id=1, source_target_pairs={{0,1},{1,2},{2,3},{3,4},{4,5},{5,6},{6,7},{7,0},{8,9},{9,10},{10,1... | collective-permute-start | bytes 6291464 | tf_op jit(solution)/shard_map/ppermute | solution.py:36
  79.9 1.3 copy-start.14
  81.2 25.5 %collective-permute-start.3 = (bf16[1,2,256,2048]{3,2,1,0:T(8,128)(2,1)S(1)}, bf16[1,2,256,2048]{3,2,1,0:T(8,128)(2,1)S(1)}, u32[]{:S(2)}, u32[]{:S(2)}) collective-permute-start(bf16[1,2,256,2048]{3,2,1,0:T(8,128)(2,1)S(1)} %collective-permute-done.2), channel_id=1, source_target_pairs={{0,1},{1,2},{2,3},{3,4},{4,5},{5,6},{6,7},{7,0},{8,9},{9,10},{10,1... | collective-permute-start | bytes 6291464 | tf_op jit(solution)/shard_map/ppermute | solution.py:36
  106.7 1.3 copy-start.16
  108.0 25.5 %collective-permute-start.4 = (bf16[1,2,256,2048]{3,2,1,0:T(8,128)(2,1)S(1)}, bf16[1,2,256,2048]{3,2,1,0:T(8,128)(2,1)S(1)}, u32[]{:S(2)}, u32[]{:S(2)}) collective-permute-start(bf16[1,2,256,2048]{3,2,1,0:T(8,128)(2,1)S(1)} %collective-permute-done.3), channel_id=1, source_target_pairs={{0,1},{1,2},{2,3},{3,4},{4,5},{5,6},{6,7},{7,0},{8,9},{9,10},{10,1... | collective-permute-start | bytes 6291464 | tf_op jit(solution)/shard_map/ppermute | solution.py:36
  133.5 1.3 copy-start.18
  134.8 25.6 %collective-permute-start.5 = (bf16[1,2,256,2048]{3,2,1,0:T(8,128)(2,1)S(1)}, bf16[1,2,256,2048]{3,2,1,0:T(8,128)(2,1)}, u32[]{:S(2)}, u32[]{:S(2)}) collective-permute-start(bf16[1,2,256,2048]{3,2,1,0:T(8,128)(2,1)S(1)} %collective-permute-done.4), channel_id=1, source_target_pairs={{0,1},{1,2},{2,3},{3,4},{4,5},{5,6},{6,7},{7,0},{8,9},{9,10},{10,1... | collective-permute-start | bytes 6291464 | tf_op jit(solution)/shard_map/ppermute | solution.py:36
  160.4 25.8 %collective-permute-start.6 = (bf16[1,2,256,2048]{3,2,1,0:T(8,128)(2,1)}, bf16[1,2,256,2048]{3,2,1,0:T(8,128)(2,1)}, u32[]{:S(2)}, u32[]{:S(2)}) collective-permute-start(bf16[1,2,256,2048]{3,2,1,0:T(8,128)(2,1)} %collective-permute-done.5), channel_id=1, source_target_pairs={{0,1},{1,2},{2,3},{3,4},{4,5},{5,6},{6,7},{7,0},{8,9},{9,10},{10,1... | collective-permute-start | bytes 6291464 | tf_op jit(solution)/shard_map/ppermute | solution.py:36
  163.2 29.6 %copy-start.19 = (bf16[1,2,256,2048]{3,2,1,0:T(8,128)(2,1)S(1)}, bf16[1,2,256,2048]{3,2,1,0:T(8,128)(2,1)}, u32[]{:S(2)}) copy-start(bf16[1,2,256,2048]{3,2,1,0:T(8,128)(2,1)} %copy-done.18) | copy-start | bytes 6291460
  189.3 5.0 copy-start.17
  192.8 3.0 copy-start.15
  194.4 3.0 copy-start.13
  195.8 3.1 copy-start.11
  197.4 3.1 copy-start.9
  235.5 6.8 %copy-start.5 = (f32[1,1,256,2048]{2,3,1,0:T(8,128)}, f32[1,1,256,2048]{2,3,1,0:T(8,128)S(1)}, u32[]{:S(2)}) copy-start(f32[1,1,256,2048]{2,3,1,0:T(8,128)S(1)} %fusion.18) | copy-start | bytes 6291460
  242.3 2.1 copy-start.7
  301.6 8.8 %copy-start.25 = (bf16[1,2,256,2048]{2,3,1,0:T(8,128)(2,1)}, bf16[1,2,256,2048]{2,3,1,0:T(8,128)(2,1)S(1)}, u32[]{:S(2)}) copy-start(bf16[1,2,256,2048]{2,3,1,0:T(8,128)(2,1)S(1)} %fusion.38) | copy-start | bytes 6291460
  320.5 7.8 %copy-start.26 = (bf16[1,2,256,2048]{2,3,1,0:T(8,128)(2,1)S(1)}, bf16[1,2,256,2048]{2,3,1,0:T(8,128)(2,1)}, u32[]{:S(2)}) copy-start(bf16[1,2,256,2048]{2,3,1,0:T(8,128)(2,1)} %copy-done.25) | copy-start | bytes 6291460
  320.5 7.8 %copy-start.27 = (f32[256,2048]{0,1:T(8,128)S(1)}, f32[256,2048]{0,1:T(8,128)}, u32[]{:S(2)}) copy-start(f32[256,2048]{0,1:T(8,128)} %fusion.27) | copy-start | bytes 6291460
  328.3 7.3 %copy-start.6 = (f32[1,1,256,2048]{2,3,1,0:T(8,128)S(1)}, f32[1,1,256,2048]{2,3,1,0:T(8,128)}, u32[]{:S(2)}) copy-start(f32[1,1,256,2048]{2,3,1,0:T(8,128)} %copy-done.5) | copy-start | bytes 6291460
  328.3 7.3 %copy-start.8 = (f32[1,1,256,2048]{2,3,1,0:T(8,128)S(1)}, f32[1,1,256,2048]{2,3,1,0:T(8,128)}, u32[]{:S(2)}) copy-start(f32[1,1,256,2048]{2,3,1,0:T(8,128)} %copy-done.7) | copy-start | bytes 6291460
  337.4 25.5 %copy-start = (f32[1,2,256,2048]{2,3,1,0:T(8,128)}, f32[1,2,256,2048]{2,3,1,0:T(8,128)S(1)}, u32[]{:S(2)}) copy-start(f32[1,2,256,2048]{2,3,1,0:T(8,128)S(1)} %get-tuple-element.33) | copy-start | bytes 12582916
  356.3 6.5 %copy-start.21 = (f32[1,1,256,2048]{2,3,1,0:T(8,128)}, f32[1,1,256,2048]{2,3,1,0:T(8,128)S(1)}, u32[]{:S(2)}) copy-start(f32[1,1,256,2048]{2,3,1,0:T(8,128)S(1)} %fusion.12) | copy-start | bytes 6291460
  362.8 4.4 copy-start.22
  432.3 7.5 %copy-start.28 = (f32[256,2048]{0,1:T(8,128)S(1)}, f32[256,2048]{0,1:T(8,128)}, u32[]{:S(2)}) copy-start(f32[256,2048]{0,1:T(8,128)} %fusion.31) | copy-start | bytes 6291460
  439.8 7.2 %copy-start.1 = (f32[1,2,256,2048]{2,3,1,0:T(8,128)S(1)}, f32[1,2,256,2048]{2,3,1,0:T(8,128)}, u32[]{:S(2)}) copy-start(f32[1,2,256,2048]{2,3,1,0:T(8,128)} %copy-done) | copy-start | bytes 12582916
  439.8 7.2 %copy-start.2 = (f32[1,2,256,2048]{2,3,1,0:T(8,128)S(1)}, f32[1,2,256,2048]{2,3,1,0:T(8,128)}, u32[]{:S(2)}) copy-start(f32[1,2,256,2048]{2,3,1,0:T(8,128)} %get-tuple-element.30) | copy-start | bytes 12582916
  449.5 7.8 %copy-start.23 = (bf16[1,2,256,2048]{2,3,1,0:T(8,128)(2,1)}, bf16[1,2,256,2048]{2,3,1,0:T(8,128)(2,1)S(1)}, u32[]{:S(2)}) copy-start(bf16[1,2,256,2048]{2,3,1,0:T(8,128)(2,1)S(1)} %get-tuple-element.27) | copy-start | bytes 6291460
  464.5 6.8 %copy-start.24 = (bf16[1,2,256,2048]{2,3,1,0:T(8,128)(2,1)S(1)}, bf16[1,2,256,2048]{2,3,1,0:T(8,128)(2,1)}, u32[]{:S(2)}) copy-start(bf16[1,2,256,2048]{2,3,1,0:T(8,128)(2,1)} %copy-done.23) | copy-start | bytes 6291460
  464.5 6.8 %copy-start.29 = (f32[256,2048]{0,1:T(8,128)S(1)}, f32[256,2048]{0,1:T(8,128)}, u32[]{:S(2)}) copy-start(f32[256,2048]{0,1:T(8,128)} %fusion.33) | copy-start | bytes 6291460
  471.3 6.1 %copy-start.3 = (f32[1,2,256,2048]{2,3,1,0:T(8,128)S(1)}, f32[1,2,256,2048]{2,3,1,0:T(8,128)}, u32[]{:S(2)}) copy-start(f32[1,2,256,2048]{2,3,1,0:T(8,128)} %get-tuple-element.30) | copy-start | bytes 12582916
  471.3 6.1 %copy-start.4 = (f32[1,2,256,2048]{2,3,1,0:T(8,128)S(1)}, f32[1,2,256,2048]{2,3,1,0:T(8,128)}, u32[]{:S(2)}) copy-start(f32[1,2,256,2048]{2,3,1,0:T(8,128)} %get-tuple-element.28) | copy-start | bytes 12582916
  477.5 2.5 copy-start.20
